TPU v7x, 256 devices: a whole 4x4x8 slice. The times are simulated.
256 devices in a mesh: rp: 8 (over x, z_lo), pb: 32 (over z_hi, y, core).
Axes of the slice: x: 4, y: 4, z: 8 (z_hi: 4, z_lo: 2; z = z_hi * 2 + z_lo), core: 2. Of those that a mesh axis runs over, the one named last changes fastest.
Arguments:
- wannier_g: bfloat16 [2, 1024, 32, 1152], P(None, 'rp', 'pb'), may hold values from -0.19921875 to 0.19921875
- rp_coords: int32 [3, 1024], replicated, may hold values from -8 to 8
- q_coords: int32 [3, 512], P(None, ('rp', 'pb')), may hold values from 0 to 15
- k_index: int32 [1], replicated, may hold values from 0 to 7
- k_vectors: bfloat16 [8, 2, 32, 32], replicated, may hold values from -0.75 to 0.75
- kq_vectors: bfloat16 [512, 2, 32, 32], P(('rp', 'pb')), may hold values from -0.75 to 0.75
- modes: bfloat16 [512, 2, 36, 36], P(('rp', 'pb')), may hold values from -0.75 to 0.75
Outputs:
- rotated: float32 [512, 2, 32, 1152], P(('rp', 'pb'))
All inputs are finite; a program needn't handle non-finite values.
Results may differ from a plain program's by a relative error of at most 0.0054.
Values may be sent and summed in bfloat16 or wider, within the bound.
A program may use at most 64 MiB of HBM per device.

v0:
```python
import math

import jax
import jax.numpy as jnp
from jax import lax
from jax.sharding import PartitionSpec as P

NK = 16


def in_blocks(x, dim, length):
    shape = x.shape
    parts = x.reshape(*shape[:dim], length, shape[dim] // length, *shape[dim + 1 :])
    return jnp.moveaxis(parts, dim, 0)


def joined_along(parts, dim):
    shape = list(parts.shape[1:])
    shape[dim] *= parts.shape[0]
    return jnp.moveaxis(parts, 0, dim).reshape(shape)


def one_exchange(x, axis, axes, splits, concats):
    sizes = [lax.axis_size(a) for a in axes]
    parts = in_blocks(x, splits[0], sizes[0])
    parts = jnp.moveaxis(in_blocks(parts, splits[1] + 1, sizes[1]), 0, 1)
    inside = parts.shape[2:]
    parts = parts.reshape(-1, *inside)
    parts = lax.all_to_all(parts, axis, split_axis=0, concat_axis=0, tiled=True)
    parts = joined_along(parts.reshape(*sizes, *inside), concats[0] + 1)
    return joined_along(parts, concats[1])


def phases(q_rows, r_coords):
    turns = jnp.mod(jnp.sum(q_rows[:, :, None] * r_coords[:, None, :], axis=0), NK)
    angle = turns.astype(jnp.float32) * (2.0 * math.pi / NK)
    cosine = jnp.cos(angle).astype(jnp.bfloat16)
    sine = jnp.sin(angle).astype(jnp.bfloat16)
    return (jnp.concatenate([cosine, -sine], axis=1), jnp.concatenate([sine, cosine], axis=1))


def rotate(fourier, mode_vecs, unit, kq_vecs):
    count = fourier.shape[0]
    bands = kq_vecs.shape[2]
    branches = mode_vecs.shape[2]
    field = fourier.reshape(count, 2, bands, bands, branches)
    e_real, e_imag = (mode_vecs[:, 0], mode_vecs[:, 1])
    e_block = jnp.stack([jnp.stack([e_real, e_imag], 2), jnp.stack([-e_imag, e_real], 2)], 1)
    by_mode = jnp.einsum(
        "qcmnv,qcvdu->qdmnu", field, e_block, preferred_element_type=jnp.float32
    ).astype(jnp.bfloat16)
    u_real, u_imag = (unit[0], unit[1])
    u_block = jnp.stack([jnp.stack([u_real, u_imag], 1), jnp.stack([-u_imag, u_real], 1)], 0)
    by_band = jnp.einsum(
        "qcmnu,cndj->qdmju", by_mode, u_block, preferred_element_type=jnp.float32
    ).astype(jnp.bfloat16)
    v_real, v_imag = (kq_vecs[:, 0], kq_vecs[:, 1])
    v_block = jnp.stack([jnp.stack([v_real, -v_imag], 2), jnp.stack([v_imag, v_real], 2)], 1)
    result = jnp.einsum("qcmju,qcmdi->qdiju", by_band, v_block, preferred_element_type=jnp.float32)
    return result.reshape(count, 2, bands, bands * branches)


def local(wannier_g, rp_coords, q_coords, k_index, k_vectors, kq_vectors, modes):
    q_all = lax.all_gather(q_coords, ("rp", "pb"), axis=1, tiled=True)
    total = q_all.shape[1]
    groups = lax.axis_size("rp")
    block = total // groups
    moved = lax.all_to_all(wannier_g, "rp", split_axis=3, concat_axis=1, tiled=True)
    right = moved.reshape(2 * moved.shape[1], -1)
    q_blocks = q_all.reshape(3, groups, block).transpose(1, 0, 2)

    def fourier_block(q_rows):
        left_real, left_imag = phases(q_rows, rp_coords)
        f_real = jnp.dot(left_real, right, preferred_element_type=jnp.float32).astype(jnp.bfloat16)
        f_imag = jnp.dot(left_imag, right, preferred_element_type=jnp.float32).astype(jnp.bfloat16)
        return jnp.stack([f_real, f_imag], 1)

    fourier = lax.map(fourier_block, q_blocks).reshape(total, 2, moved.shape[2], moved.shape[3])
    owned = one_exchange(fourier, ("rp", "pb"), ("rp", "pb"), (0, 0), (3, 2))
    select = (jnp.arange(k_vectors.shape[0]) == k_index[0]).astype(jnp.bfloat16)
    unit = jnp.einsum("k,kcnj->cnj", select, k_vectors, preferred_element_type=jnp.float32).astype(
        jnp.bfloat16
    )
    return rotate(owned, modes, unit, kq_vectors)


def solution(mesh):
    return jax.shard_map(
        local,
        mesh=mesh,
        in_specs=(
            P(None, "rp", "pb", None),
            P(),
            P(None, ("rp", "pb")),
            P(),
            P(),
            P(("rp", "pb"), None, None, None),
            P(("rp", "pb"), None, None, None),
        ),
        out_specs=P(("rp", "pb"), None, None, None),
        check_vma=False,
    )
```

profile of v0, /device:TPU:1, one launch (start us, length us, event | category | flops | bytes accessed | tf_op | source)
XLA Modules:
  0.0 424.2 jit_solution(9630580377085636037)
XLA Ops:
  0.0 3.0 copy.101
  3.0 6.2 %all-to-all-start = ((bf16[2,128,1,1152]{1,0,2,3:T(2,128)(2,1)}), bf16[2,128,1,1152]{1,0,2,3:T(2,128)(2,1)S(1)}, u32[]{:S(2)}, u32[]{:S(2)}) async-start(bf16[2,128,1,1152]{1,0,2,3:T(2,128)(2,1)} %copy.101), calls=%async_computation | async-start | bytes 1179648 | tf_op jit(solution)/shard_map/all_to_all | solution.py:68
  10.3 350.8 %all-gather = s32[256,2,3]{2,1,0:T(2,128)S(1)} all-gather(s32[1,2,3]{2,1,0:T(2,128)S(1)} %bitcast.145), channel_id=1, replica_groups=mesh['rp'=8,'pb'=32] {'rp','pb'}, dimensions={0}, use_global_device_ids=true | all-gather | bytes 6168 | tf_op jit(solution)/shard_map/all_gather | solution.py:64
  361.4 0.5 copy.128
  362.0 27.2 %while.12 = (s32[]{:T(128)}, bf16[8,64,2,144]{3,2,1,0:T(2,128)(2,1)}, s32[8,3,64]{2,0,1:T(8,128)S(1)}, s32[3,1024]{1,0:T(4,128)S(1)}, bf16[2048,144]{1,0:T(8,128)(2,1)S(1)}, /*index=5*/s32[]{:T(128)}) while((s32[]{:T(128)}, bf16[8,64,2,144]{3,2,1,0:T(2,128)(2,1)}, s32[8,3,64]{2,0,1:T(8,128)S(1)}, s32[3,1024]{1,0:T(4,128)S(1)}, ...), condition=%wide.region_2.3_spmd, body=%wide.region_0.2_spmd.sunk | while | flops 78942208 | bytes 3112789 | solution.py:78
  362.1 0.9 cosine_convert_fusion.2
  363.1 1.0 fusion.51
  364.4 0.3 fusion.53
  364.7 0.7 copy_dynamic-update-slice_fusion.2
  365.5 0.9 cosine_convert_fusion.2
  366.5 1.0 fusion.51
  367.4 0.3 fusion.52
  368.1 0.7 copy_dynamic-update-slice_fusion.2
  368.9 0.9 cosine_convert_fusion.2
  369.9 1.0 fusion.51
  371.1 0.3 fusion.53
  371.5 0.7 copy_dynamic-update-slice_fusion.2
  372.3 0.9 cosine_convert_fusion.2
  373.3 1.0 fusion.51
  374.5 0.3 fusion.53
  374.9 0.7 copy_dynamic-update-slice_fusion.2
  375.7 0.9 cosine_convert_fusion.2
  376.6 1.0 fusion.51
  377.6 0.3 fusion.52
  378.2 0.7 copy_dynamic-update-slice_fusion.2
  379.1 0.9 cosine_convert_fusion.2
  380.0 1.0 fusion.51
  381.3 0.3 fusion.53
  381.6 0.7 copy_dynamic-update-slice_fusion.2
  382.5 0.9 cosine_convert_fusion.2
  383.4 1.0 fusion.51
  384.4 0.3 fusion.52
  384.7 0.3 fusion.53
  385.0 0.7 copy_dynamic-update-slice_fusion.2
  385.9 0.9 cosine_convert_fusion.2
  386.8 1.0 fusion.51
  387.8 0.3 fusion.52
  388.4 0.7 copy_dynamic-update-slice_fusion.2
  389.1 5.3 %all-to-all-start.1 = ((bf16[256,2,2,1,144]{4,2,1,3,0:T(2,128)(2,1)}), bf16[256,2,2,1,144]{4,2,1,3,0:T(2,128)(2,1)S(1)}, u32[]{:S(2)}, u32[]{:S(2)}) async-start(bf16[256,2,2,1,144]{4,2,1,3,0:T(2,128)(2,1)} %bitcast.38), calls=%async_computation.1 | async-start | bytes 1048576 | tf_op jit(solution)/shard_map/all_to_all | solution.py:29
  394.9 20.4 %all-to-all-done.1 = bf16[256,2,2,1,144]{4,2,1,3,0:T(2,128)(2,1)S(1)} async-done(((bf16[256,2,2,1,144]{4,2,1,3,0:T(2,128)(2,1)}), bf16[256,2,2,1,144]{4,2,1,3,0:T(2,128)(2,1)S(1)}, u32[]{:S(2)}, u32[]{:S(2)}) %all-to-all-start.1) | async-done | bytes 294944 | tf_op jit(solution)/shard_map/all_to_all | solution.py:29
  415.4 0.3 copy.109
  415.7 0.5 reshape.52
  416.2 2.8 reshape_reshape.3
  419.0 0.5 fusion.13
  419.5 0.5 fusion.14
  420.0 0.5 convolution_bitcast_fusion
  420.5 1.2 copy.114
  421.7 2.4 reshape.53
  (70 shorter events, 4.5 us)
Async XLA Ops:
  0.0 9.9 %copy-start = (bf16[8,2,32,32]{3,2,1,0:T(8,128)(2,1)S(1)}, bf16[8,2,32,32]{3,2,1,0:T(8,128)(2,1)}, u32[]{:S(2)}) copy-start(bf16[8,2,32,32]{3,2,1,0:T(8,128)(2,1)} %param.13) | copy-start | bytes 98308
  0.0 10.2 %copy-start.3 = (bf16[2,2,32,32]{3,2,1,0:T(8,128)(2,1)S(1)}, bf16[2,2,32,32]{3,2,1,0:T(8,128)(2,1)}, u32[]{:S(2)}) copy-start(bf16[2,2,32,32]{3,2,1,0:T(8,128)(2,1)} %param.14) | copy-start | bytes 24580
  0.0 10.3 %copy-start.4 = (s32[3,2]{0,1:T(2,128)S(1)}, s32[3,2]{0,1:T(2,128)}, u32[]{:S(2)}) copy-start(s32[3,2]{0,1:T(2,128)} %param.11) | copy-start | bytes 76
  0.0 361.3 %copy-start.2 = (bf16[2,2,36,36]{3,1,2,0:T(2,128)(2,1)S(1)}, bf16[2,2,36,36]{3,1,2,0:T(2,128)(2,1)}, u32[]{:S(2)}) copy-start(bf16[2,2,36,36]{3,1,2,0:T(2,128)(2,1)} %param.15) | copy-start | bytes 31108
  3.0 358.3 %all-to-all-start = ((bf16[2,128,1,1152]{1,0,2,3:T(2,128)(2,1)}), bf16[2,128,1,1152]{1,0,2,3:T(2,128)(2,1)S(1)}, u32[]{:S(2)}, u32[]{:S(2)}) async-start(bf16[2,128,1,1152]{1,0,2,3:T(2,128)(2,1)} %copy.101), calls=%async_computation | async-start | bytes 1179648 | tf_op jit(solution)/shard_map/all_to_all | solution.py:68
  9.2 352.8 %copy-start.1 = (s32[3,1024]{1,0:T(4,128)S(1)}, s32[3,1024]{1,0:T(4,128)}, u32[]{:S(2)}) copy-start(s32[3,1024]{1,0:T(4,128)} %param.10) | copy-start | bytes 36868
  389.1 26.2 %all-to-all-start.1 = ((bf16[256,2,2,1,144]{4,2,1,3,0:T(2,128)(2,1)}), bf16[256,2,2,1,144]{4,2,1,3,0:T(2,128)(2,1)S(1)}, u32[]{:S(2)}, u32[]{:S(2)}) async-start(bf16[256,2,2,1,144]{4,2,1,3,0:T(2,128)(2,1)} %bitcast.38), calls=%async_computation.1 | async-start | bytes 1048576 | tf_op jit(solution)/shard_map/all_to_all | solution.py:29
where the time goes:
time: 424 us
  blocking collectives  351 us (83%)
  waiting for transfers between devices  20.4 us (5%)
  local copies, waits for them, and re-layouts  17 us (4%)
  other arithmetic  16.8 us (4%)
  starting transfers between devices  11.5 us (3%)
  matrix products  6.36 us (2%)
    all_gather x1, blocking collectives, local(): q_all = lax.all_gather(q_coords, ('rp', 'pb'), axis=1, tiled=True)  351 us
    all_to_all x1, waiting for transfers between devices, one_exchange(): parts = lax.all_to_all(parts, axis, split_axis=0, concat_axis=0, tiled=True)  20.4 us
  transfers between devices with their start and end apart: 2, of which 1 were waited for; matrix products, arithmetic and copies ran while one was open for 0% of the time, Pallas kernels for 0%

commit v1 on v0

--- a/solution.py
+++ b/solution.py
@@ -1,9 +1,14 @@
+import functools
 import math
 
 import jax
 import jax.numpy as jnp
 from jax import lax
+from jax.experimental import pallas as pl
+from jax.experimental.pallas import tpu as pltpu
 from jax.sharding import PartitionSpec as P
+
+MESH = pl.DeviceIdType.MESH
 
 NK = 16
 
@@ -29,6 +34,58 @@
     parts = lax.all_to_all(parts, axis, split_axis=0, concat_axis=0, tiled=True)
     parts = joined_along(parts.reshape(*sizes, *inside), concats[0] + 1)
     return joined_along(parts, concats[1])
+
+
+def gather_kernel(n_rp, n_pb, x_ref, o_ref, send_sem, recv_sem):
+    rp, pb = lax.axis_index("rp"), lax.axis_index("pb")
+    me = rp * n_pb + pb
+    total = n_rp * n_pb
+    barrier = pltpu.get_barrier_semaphore()
+
+    def greet(step, carry):
+        other = lax.rem(me + step, total)
+        pl.semaphore_signal(
+            barrier, inc=1, device_id=(other // n_pb, lax.rem(other, n_pb)), device_id_type=MESH
+        )
+        return carry
+
+    lax.fori_loop(1, total, greet, 0)
+    pl.semaphore_wait(barrier, total - 1)
+
+    def push(step, carry):
+        other = lax.rem(me + step, total)
+        pltpu.make_async_remote_copy(
+            src_ref=x_ref,
+            dst_ref=o_ref.at[me],
+            send_sem=send_sem,
+            recv_sem=recv_sem,
+            device_id=(other // n_pb, lax.rem(other, n_pb)),
+            device_id_type=MESH,
+        ).start()
+        return carry
+
+    lax.fori_loop(1, total, push, 0)
+    rest = o_ref.at[pl.ds(0, total - 1)]
+    pltpu.make_async_copy(rest, rest, recv_sem).wait()
+    pltpu.make_async_copy(rest, rest, send_sem).wait()
+    o_ref[me] = x_ref[...]
+
+
+def gather_coords(q_coords):
+    n_rp, n_pb = lax.axis_size("rp"), lax.axis_size("pb")
+    own = q_coords.shape[1]
+    row = jnp.pad(q_coords.reshape(1, -1), ((0, 0), (0, 128 - 3 * own)))
+    gathered = pl.pallas_call(
+        functools.partial(gather_kernel, n_rp, n_pb),
+        name="gather_coords",
+        out_shape=jax.ShapeDtypeStruct((n_rp * n_pb, 1, 128), jnp.int32),
+        in_specs=[pl.BlockSpec(memory_space=pltpu.VMEM)],
+        out_specs=pl.BlockSpec(memory_space=pltpu.VMEM),
+        scratch_shapes=[pltpu.SemaphoreType.DMA, pltpu.SemaphoreType.DMA],
+        compiler_params=pltpu.CompilerParams(collective_id=0, has_side_effects=True),
+    )(row)
+    coords = gathered[:, 0, : 3 * own].reshape(-1, 3, own)
+    return coords.transpose(1, 0, 2).reshape(3, -1)
 
 
 def phases(q_rows, r_coords):
@@ -61,7 +118,7 @@
 
 
 def local(wannier_g, rp_coords, q_coords, k_index, k_vectors, kq_vectors, modes):
-    q_all = lax.all_gather(q_coords, ("rp", "pb"), axis=1, tiled=True)
+    q_all = gather_coords(q_coords)
     total = q_all.shape[1]
     groups = lax.axis_size("rp")
     block = total // groups

time: 424 us -> 105 us (0.25)
  blocking collectives: 351 us -> 0 us
  Pallas kernels: 0 us -> 24.1 us
  starting transfers between devices: 11.5 us -> 17 us
    all_gather x1 -> x0, blocking collectives: 351 us -> none  [local(): q_all = lax.all_gather(q_coords, ('rp', 'pb'), axis=1, tiled=True)]
    pallas_call x0 -> x1, Pallas kernels: none -> 24.1 us  [gather_coords(): pl.pallas_call(functools.partial(gather_kernel, n_rp, n_pb), name='gather...]
    all_to_all x1, starting transfers between devices: 5.34 us -> 10.8 us  [one_exchange(): parts = lax.all_to_all(parts, axis, split_axis=0, concat_axis=0, tiled=True)]
  transfers between devices with their start and end apart: 2 -> 2, of which waited for: 1 -> 1; matrix products, arithmetic and copies ran while one was open for 0% -> 3% of each run, Pallas kernels for 0% -> 23%
where the time goes in v1:
time: 105 us
  Pallas kernels  24.1 us (23%)
  waiting for transfers between devices  20.5 us (20%)
  local copies, waits for them, and re-layouts  19 us (18%)
  starting transfers between devices  17 us (16%)
  other arithmetic  16.8 us (16%)
  matrix products  6.36 us (6%)
    pallas_call x1, Pallas kernels, gather_coords(): pl.pallas_call(functools.partial(gather_kernel, n_rp, n_pb), name='gather...  24.1 us
    all_to_all x1, waiting for transfers between devices, one_exchange(): parts = lax.all_to_all(parts, axis, split_axis=0, concat_axis=0, tiled=True)  20.5 us
    all_to_all x1, starting transfers between devices, one_exchange(): parts = lax.all_to_all(parts, axis, split_axis=0, concat_axis=0, tiled=True)  10.8 us
    neg x8, other arithmetic, phases(): -sine  7.76 us
    convert_element_type x8, other arithmetic, phases(): cosine = jnp.cos(angle).astype(jnp.bfloat16)  7.6 us
    all_to_all x1, starting transfers between devices, local(): lax.all_to_all(wannier_g, 'rp', split_axis=3, concat_axis=1, tiled=True)  6.19 us
    dynamic_update_slice x8, local copies, waits for them, and re-layouts, local(): lax.map(fourier_block, q_blocks)  5.54 us
    unnamed x15, local copies, waits for them, and re-layouts  3.32 us
  transfers between devices with their start and end apart: 2, of which 1 were waited for; matrix products, arithmetic and copies ran while one was open for 3% of the time, Pallas kernels for 23%

profile of v1, /device:TPU:1, one launch (start us, length us, event | category | flops | bytes accessed | tf_op | source)
XLA Modules:
  0.0 105.0 jit_solution(4171846356502646276)
XLA Ops:
  0.0 3.0 %copy.112 = bf16[2,128,1,1152]{1,0,2,3:T(2,128)(2,1)} copy(bf16[2,128,1,1152]{3,1,2,0:T(8,128)(2,1)} %param.9) | data formatting | bytes 1179648 | tf_op args[0]
  3.0 6.2 %all-to-all-start = ((bf16[2,128,1,1152]{1,0,2,3:T(2,128)(2,1)}), bf16[2,128,1,1152]{1,0,2,3:T(2,128)(2,1)S(1)}, u32[]{:S(2)}, u32[]{:S(2)}) async-start(bf16[2,128,1,1152]{1,0,2,3:T(2,128)(2,1)} %copy.112), calls=%async_computation | async-start | bytes 1179648 | tf_op jit(solution)/shard_map/all_to_all | solution.py:125
  10.5 0.6 pad.4.x_ref
  11.1 24.1 %gather_coords.1 = s32[256,1,128]{2,1,0:T(1,128)} custom-call(s32[1,128]{1,0:T(1,128)} %pad.4.x_ref), custom_call_target="tpu_custom_call" | custom-call | tf_op jit(solution)/shard_map/gather_coords/pallas_call | solution.py:78
  35.2 1.0 copy.110
  36.8 0.5 copy.139
  37.3 27.2 %while.12 = (s32[]{:T(128)}, bf16[8,64,2,144]{3,2,1,0:T(2,128)(2,1)}, s32[8,3,64]{2,0,1:T(8,128)S(1)}, s32[3,1024]{1,0:T(4,128)S(1)}, bf16[2048,144]{1,0:T(8,128)(2,1)S(1)}, /*index=5*/s32[]{:T(128)}) while((s32[]{:T(128)}, bf16[8,64,2,144]{3,2,1,0:T(2,128)(2,1)}, s32[8,3,64]{2,0,1:T(8,128)S(1)}, s32[3,1024]{1,0:T(4,128)S(1)}, ...), condition=%wide.region_2.3_spmd, body=%wide.region_0.2_spmd.sunk | while | flops 78942208 | bytes 3112789 | solution.py:135
  37.5 0.9 cosine_convert_fusion.2
  38.5 1.0 fusion.51
  40.1 0.7 copy_dynamic-update-slice_fusion.2
  40.9 0.9 cosine_convert_fusion.2
  41.8 1.0 fusion.51
  43.1 0.3 fusion.53
  43.4 0.7 copy_dynamic-update-slice_fusion.2
  44.3 0.9 cosine_convert_fusion.2
  45.2 1.0 fusion.51
  46.8 0.7 copy_dynamic-update-slice_fusion.2
  47.7 0.9 cosine_convert_fusion.2
  48.6 1.0 fusion.51
  49.6 0.3 fusion.52
  50.2 0.7 copy_dynamic-update-slice_fusion.2
  51.1 0.9 cosine_convert_fusion.2
  52.0 1.0 fusion.51
  53.0 0.3 fusion.52
  53.6 0.7 copy_dynamic-update-slice_fusion.2
  54.5 0.9 cosine_convert_fusion.2
  55.4 1.0 fusion.51
  56.7 0.3 fusion.53
  57.0 0.7 copy_dynamic-update-slice_fusion.2
  57.8 0.9 cosine_convert_fusion.2
  58.8 1.0 fusion.51
  59.8 0.3 fusion.52
  60.1 0.3 fusion.53
  60.4 0.7 copy_dynamic-update-slice_fusion.2
  61.2 0.9 cosine_convert_fusion.2
  62.2 1.0 fusion.51
  63.2 0.3 fusion.52
  63.8 0.7 copy_dynamic-update-slice_fusion.2
  64.5 10.8 %all-to-all-start.1 = ((bf16[256,2,2,1,144]{4,2,1,3,0:T(2,128)(2,1)}), bf16[256,2,2,1,144]{4,2,1,3,0:T(2,128)(2,1)S(1)}, u32[]{:S(2)}, u32[]{:S(2)}) async-start(bf16[256,2,2,1,144]{4,2,1,3,0:T(2,128)(2,1)} %bitcast.35), calls=%async_computation.1 | async-start | bytes 1048576 | tf_op jit(solution)/shard_map/all_to_all | solution.py:34
  75.7 20.5 %all-to-all-done.1 = bf16[256,2,2,1,144]{4,2,1,3,0:T(2,128)(2,1)S(1)} async-done(((bf16[256,2,2,1,144]{4,2,1,3,0:T(2,128)(2,1)}), bf16[256,2,2,1,144]{4,2,1,3,0:T(2,128)(2,1)S(1)}, u32[]{:S(2)}, u32[]{:S(2)}) %all-to-all-start.1) | async-done | bytes 294944 | tf_op jit(solution)/shard_map/all_to_all | solution.py:34
  96.3 0.3 copy.120
  96.6 0.5 reshape.52
  97.0 2.8 %reshape_reshape.7 = bf16[2,2,32,32,36]{4,3,2,1,0:T(8,128)(2,1)S(1)} reshape(bf16[2,2,32,1,1152]{4,2,1,0,3:T(8,128)(2,1)S(1)} %bitcast.134) | data formatting | bytes 589824 | tf_op jit(solution)/shard_map/reshape;reshape | solution.py:103
  99.8 0.5 fusion.13
  100.3 0.5 fusion.14
  100.8 0.5 convolution_bitcast_fusion
  101.3 1.2 %copy.125 = f32[2,2,32,32,36]{4,3,2,1,0:T(8,128)S(1)} copy(f32[2,2,32,32,36]{4,2,3,1,0:T(8,128)S(1)} %convolution_bitcast_fusion) | data formatting | bytes 1179648 | tf_op jit(solution)/shard_map/qcmju,qcmdi->qdiju/dot_general | solution.py:116
  102.6 2.4 %reshape.53 = f32[2,2,32,1152]{3,2,1,0:T(8,128)} reshape(f32[2,2,32,32,36]{4,3,2,1,0:T(8,128)S(1)} %copy.125) | data formatting | bytes 1179648 | tf_op jit(solution)/shard_map/reshape | solution.py:117
  (75 shorter events, 5.5 us)
Async XLA Ops:
  0.0 10.1 %copy-start = (bf16[8,2,32,32]{3,2,1,0:T(8,128)(2,1)S(1)}, bf16[8,2,32,32]{3,2,1,0:T(8,128)(2,1)}, u32[]{:S(2)}) copy-start(bf16[8,2,32,32]{3,2,1,0:T(8,128)(2,1)} %param.13) | copy-start | bytes 98308
  0.0 9.9 %copy-start.4 = (s32[3,2]{0,1:T(2,128)S(1)}, s32[3,2]{0,1:T(2,128)}, u32[]{:S(2)}) copy-start(s32[3,2]{0,1:T(2,128)} %param.11) | copy-start | bytes 76
  0.0 10.3 %copy-start.3 = (bf16[2,2,32,32]{3,2,1,0:T(8,128)(2,1)S(1)}, bf16[2,2,32,32]{3,2,1,0:T(8,128)(2,1)}, u32[]{:S(2)}) copy-start(bf16[2,2,32,32]{3,2,1,0:T(8,128)(2,1)} %param.14) | copy-start | bytes 24580
  0.0 36.6 %copy-start.2 = (bf16[2,2,36,36]{3,1,2,0:T(2,128)(2,1)S(1)}, bf16[2,2,36,36]{3,1,2,0:T(2,128)(2,1)}, u32[]{:S(2)}) copy-start(bf16[2,2,36,36]{3,1,2,0:T(2,128)(2,1)} %param.15) | copy-start | bytes 31108
  3.0 33.7 %all-to-all-start = ((bf16[2,128,1,1152]{1,0,2,3:T(2,128)(2,1)}), bf16[2,128,1,1152]{1,0,2,3:T(2,128)(2,1)S(1)}, u32[]{:S(2)}, u32[]{:S(2)}) async-start(bf16[2,128,1,1152]{1,0,2,3:T(2,128)(2,1)} %copy.112), calls=%async_computation | async-start | bytes 1179648 | tf_op jit(solution)/shard_map/all_to_all | solution.py:125
  10.4 27.0 %copy-start.1 = (s32[3,1024]{1,0:T(4,128)S(1)}, s32[3,1024]{1,0:T(4,128)}, u32[]{:S(2)}) copy-start(s32[3,1024]{1,0:T(4,128)} %param.10) | copy-start | bytes 36868
  64.5 31.7 %all-to-all-start.1 = ((bf16[256,2,2,1,144]{4,2,1,3,0:T(2,128)(2,1)}), bf16[256,2,2,1,144]{4,2,1,3,0:T(2,128)(2,1)S(1)}, u32[]{:S(2)}, u32[]{:S(2)}) async-start(bf16[256,2,2,1,144]{4,2,1,3,0:T(2,128)(2,1)} %bitcast.35), calls=%async_computation.1 | async-start | bytes 1048576 | tf_op jit(solution)/shard_map/all_to_all | solution.py:34

commit v2 on v0

v2 whole, which is shorter than its diff:
```python
import functools
import math

import jax
import jax.numpy as jnp
from jax import lax
from jax.experimental import pallas as pl
from jax.experimental.pallas import tpu as pltpu
from jax.sharding import PartitionSpec as P

MESH = pl.DeviceIdType.MESH
F32 = jnp.float32
BF16 = jnp.bfloat16
NK = 16
N_RP = 8
N_PB = 32
N_FAR = 4
N_NEAR = 8
N_DEV = N_RP * N_PB
NB = 32
NM = 36
COLS = NB * NM
R_DEV = 128
LANES = 128
TILES = COLS // LANES
K_ALL = 2 * R_DEV * N_RP
BANDS = tuple(
    (256 * t, min(256, COLS - 256 * t), max(0, 256 * t - 128), min(COLS, 256 * t + 384)) for t in range(5)
)


def iota(shape, dim):
    return lax.broadcasted_iota(jnp.int32, shape, dim)


def band_of(x):
    return lax.shift_right_logical(x * 1821, 16)


def dot(a, b):
    return jnp.dot(a, b, preferred_element_type=F32)


def tdot(a, b):
    return lax.dot_general(a, b, (((0,), (0,)), ((), ())), preferred_element_type=F32)


def onehot(cond):
    return jnp.where(cond, 1.0, 0.0).astype(BF16)


def kernel(
    w_hbm, rc_ref, q_ref, ki_ref, kv_ref, kq_ref, e_ref, out_ref,
    wv, wr, wr2, q1, q2, ba, ph, s1, s2, rv, vb, ku, ke, y2, z2,
    w_sem, q_send, q_recv, w_send, w_recv, f_send, f_recv,
):
    rp, pb = lax.axis_index("rp"), lax.axis_index("pb")
    far, near = pb // N_NEAR, lax.rem(pb, N_NEAR)
    y_at, core = near // 2, lax.rem(near, 2)
    hot_even = 2 * lax.rem(y_at + far, 4) + lax.rem(y_at + far // 2, 2)
    hot_odd = lax.rem(hot_even + 4, 8) + 1 - 2 * lax.rem(hot_even, 2)
    hot = jnp.where(core == 0, hot_even, hot_odd)
    is_hot = rp == hot

    load = pltpu.make_async_copy(w_hbm, wv, w_sem)
    load.start()

    rp_peers = [lax.rem(rp + d, N_RP) for d in range(1, N_RP)]
    near_peers = [far * N_NEAR + lax.rem(near + d, N_NEAR) for d in range(1, N_NEAR)]
    far_peers = [lax.rem(far + d, N_FAR) * N_NEAR + near for d in range(1, N_FAR)]
    barrier = pltpu.get_barrier_semaphore()
    for other in rp_peers:
        pl.semaphore_signal(barrier, inc=1, device_id=(other, pb), device_id_type=MESH)
    for other in near_peers + far_peers:
        pl.semaphore_signal(barrier, inc=1, device_id=(rp, other), device_id_type=MESH)

    lane, row = iota((8, LANES), 1), iota((8, LANES), 0)
    k = lane - 16 * rp
    tile = jnp.where((k == 3) & (row % 2 == 1), 12.0, 0.0) + jnp.where(k == 4, 1.0, 0.0)
    for ql in range(2):
        for axis in range(3):
            value = q_ref[ql, axis].astype(F32)
            tile = tile + jnp.where((k == axis) & (row // 2 == ql), value, 0.0)
    q1[rp] = tile[:4].astype(BF16)

    pl.semaphore_wait(barrier, (N_RP - 1) + (N_NEAR - 1) + (N_FAR - 1))

    for other in rp_peers:
        pltpu.make_async_remote_copy(
            q1.at[rp], q1.at[rp], q_send.at[0], q_recv.at[0], device_id=(other, pb), device_id_type=MESH
        ).start()
    load.wait()
    for other in rp_peers:
        columns = pl.ds(pl.multiple_of(other * LANES, LANES), LANES)
        pltpu.make_async_remote_copy(
            wv.at[:, :, columns], wr.at[rp], w_send.at[0], w_recv.at[0], device_id=(other, pb), device_id_type=MESH
        ).start()
    last = wv.at[:, :, pl.ds((TILES - 1) * LANES, LANES)]

    @pl.when(jnp.logical_not(is_hot))
    def _():
        pltpu.make_async_remote_copy(
            last, wr2.at[rp], w_send.at[1], w_recv.at[1], device_id=(hot, pb), device_id_type=MESH
        ).start()

    row = iota((16, LANES), 0)
    for p in range(N_RP):
        r_at = pl.ds(p * R_DEV, R_DEV)
        for c in range(2):
            block = jnp.where(row == 3, 1.0, 0.0) + jnp.where(row == 4, 4.0 * c, 0.0)
            for axis in range(3):
                block = block + jnp.where(row == axis, rc_ref[axis : axis + 1, r_at].astype(F32), 0.0)
            at = pl.ds((2 * p + c) * R_DEV, R_DEV)
            for g in range(N_RP):
                ba[16 * g : 16 * g + 16, at] = block.astype(BF16)

    wr[rp] = wv[:, :, pl.ds(pl.multiple_of(rp * LANES, LANES), LANES)]

    @pl.when(is_hot)
    def _():
        wr2[rp] = wv[:, :, pl.ds((TILES - 1) * LANES, LANES)]

    for ql in range(2):
        col = iota((NB, LANES), 1) - 4 * iota((NB, LANES), 0)
        place = [onehot(col == 2 * ql + c) for c in range(2)]
        v = [kq_ref[ql, c] for c in range(2)]
        top = tdot(v[0], place[0]) + tdot(v[1], place[1])
        low = tdot(v[0], place[1]) - tdot(v[1], place[0])
        at = 64 * ql
        vb[at : at + 32] = top.astype(BF16)
        vb[at + 32 : at + 64] = low.astype(BF16)
        vb[128 + at : 128 + at + 32] = (-low).astype(BF16)
        vb[128 + at + 32 : 128 + at + 64] = top.astype(BF16)

    unit = kv_ref[ki_ref[0]]
    c_col = iota((NB, COLS), 1)
    spread = onehot(band_of(c_col) == iota((NB, COLS), 0))
    uc = [dot(unit[c], spread).astype(BF16) for c in range(2)]

    def band_rows(b, carry):
        start = pl.multiple_of(b * LANES, LANES)
        r = start + iota((LANES, 1), 0)
        pick = onehot(band_of(start + iota((LANES, NB), 0)) == iota((LANES, NB), 1))
        r_mode = r - NM * band_of(r)
        col = iota((1, COLS), 1)
        same = r_mode == col - NM * band_of(col)
        for c in range(2):
            full = dot(pick, uc[c])
            ku[pl.ds(c * COLS + start, LANES), :] = jnp.where(same, full, 0.0).astype(BF16)
        return carry

    lax.fori_loop(0, COLS // LANES, band_rows, 0)

    pltpu.make_async_copy(q1.at[pl.ds(0, N_RP - 1)], q1.at[pl.ds(0, N_RP - 1)], q_recv.at[0]).wait()
    q2[pb] = jnp.sum(q1[...].astype(F32), axis=0).astype(BF16)
    for other in near_peers:
        pltpu.make_async_remote_copy(
            q2.at[pb], q2.at[pb], q_send.at[1], q_recv.at[1], device_id=(rp, other), device_id_type=MESH
        ).start()

    def branch_rows(ql):
        mode_col = iota((NM, COLS), 1)
        spread_m = onehot(mode_col - NM * band_of(mode_col) == iota((NM, COLS), 0))
        ec = [dot(e_ref[ql, c], spread_m).astype(BF16) for c in range(2)]
        for t, (c0, width, r0, r1) in enumerate(BANDS):
            rows = r1 - r0
            r = r0 + iota((rows, NM), 0)
            pick = onehot(r - NM * band_of(r) == iota((rows, NM), 1))
            same = band_of(r0 + iota((rows, 1), 0)) == band_of(c0 + iota((1, width), 1))
            for c in range(2):
                full = dot(pick, ec[c][:, c0 : c0 + width])
                ke[ql, t, c * rows : (c + 1) * rows, 0:width] = jnp.where(same, full, 0.0).astype(BF16)

    branch_rows(0)

    pltpu.make_async_copy(q2.at[pl.ds(0, N_NEAR - 1)], q2.at[pl.ds(0, N_NEAR - 1)], q_recv.at[1]).wait()
    own_far = q2.at[pl.ds(far * N_NEAR, N_NEAR)]
    for other in far_peers:
        pltpu.make_async_remote_copy(
            own_far, own_far, q_send.at[2], q_recv.at[2], device_id=(rp, other), device_id_type=MESH
        ).start()

    table = jnp.cos((iota((8, LANES), 1) % NK).astype(F32) * (2.0 * math.pi / NK))
    table = jnp.broadcast_to(table[0:1], (256, LANES))

    def fill_phases(z):
        some = q2[pl.ds(z * N_NEAR, N_NEAR)].astype(F32).reshape(4 * N_NEAR, LANES)
        group = iota((4 * N_NEAR, LANES), 1) // 16
        left = jnp.concatenate([jnp.where(group == g, some, 0.0) for g in range(N_RP)], axis=0).astype(BF16)

        def columns(p, carry):
            for c in range(2):
                at = pl.ds(pl.multiple_of((2 * p + c) * LANES, LANES), LANES)
                turns = dot(left, ba[:, at]).astype(jnp.int32) & (NK - 1)
                ph[z, :, at] = jnp.take_along_axis(table, turns, axis=1, mode="promise_in_bounds").astype(BF16)
            return carry

        lax.fori_loop(0, N_RP, columns, 0)

    fill_phases(far)
    branch_rows(1)

    pltpu.make_async_copy(
        q2.at[pl.ds(0, (N_FAR - 1) * N_NEAR)], q2.at[pl.ds(0, (N_FAR - 1) * N_NEAR)], q_recv.at[2]
    ).wait()
    for d in range(1, N_FAR):
        fill_phases(lax.rem(far + d, N_FAR))

    pltpu.make_async_copy(wr.at[pl.ds(0, N_RP - 1)], wr.at[pl.ds(0, N_RP - 1)], w_recv.at[0]).wait()

    @pl.when(is_hot)
    def _():
        pltpu.make_async_copy(wr2.at[pl.ds(0, N_RP - 1)], wr2.at[pl.ds(0, N_RP - 1)], w_recv.at[1]).wait()

    mine = rp * N_NEAR + near

    def send_plane(z, first, src, slot, sem):
        def push(step, carry):
            other = lax.rem(mine + step, N_RP * N_NEAR)
            pltpu.make_async_remote_copy(
                src.at[z, other],
                rv.at[slot],
                f_send.at[sem],
                f_recv.at[sem],
                device_id=(other // N_NEAR, z * N_NEAR + lax.rem(other, N_NEAR)),
                device_id_type=MESH,
            ).start()
            return carry

        lax.fori_loop(first, N_RP * N_NEAR, push, 0)

    for d in range(N_FAR):
        z = lax.rem(far + d, N_FAR)
        part = dot(ph[z], wr[...].reshape(K_ALL, LANES))
        s1[z] = part.astype(BF16).reshape(N_RP * N_NEAR, 4, LANES)

        @pl.when(is_hot)
        def _():
            part = dot(ph[z], wr2[...].reshape(K_ALL, LANES))
            s2[z] = part.astype(BF16).reshape(N_RP * N_NEAR, 4, LANES)

        send_plane(z, 1 if d == 0 else 0, s1, rp * N_PB + pb, 0)

        @pl.when(is_hot)
        def _():
            send_plane(z, 1 if d == 0 else 0, s2, N_RP * N_PB + pb, 1)

    rv[rp * N_PB + pb] = s1[far, mine]

    @pl.when(is_hot)
    def _():
        rv[N_RP * N_PB + pb] = s2[far, mine]

    def wait_blocks(count, sem):
        pltpu.make_async_copy(rv.at[pl.ds(0, count)], rv.at[pl.ds(0, count)], sem).wait()

    wait_blocks(N_DEV - 1, f_recv.at[0])

    @pl.when(is_hot)
    def _():
        wait_blocks(N_PB - 1, f_recv.at[1])

    @pl.when(jnp.logical_not(is_hot))
    def _():
        wait_blocks(N_PB, f_recv.at[1])

    for t in range(TILES):
        got = rv[t * N_PB : (t + 1) * N_PB].reshape(4 * N_PB, LANES)
        both = dot(vb[...], got).astype(BF16)
        y2[:, t * LANES : (t + 1) * LANES] = both[:128]
        y2[:, COLS + t * LANES : COLS + (t + 1) * LANES] = both[128:]
    for t in range(5):
        c0, width = BANDS[t][:2]
        part = dot(y2[...], ku[:, c0 : c0 + width])
        z2[0, :, c0 : c0 + width] = part.astype(BF16)
        for ql in range(2):
            at = 64 * ql
            z2[1, at : at + 32, c0 : c0 + width] = (-part[at + 32 : at + 64]).astype(BF16)
            z2[1, at + 32 : at + 64, c0 : c0 + width] = part[at : at + 32].astype(BF16)
    for ql in range(2):
        rows = slice(64 * ql, 64 * ql + 64)
        for t, (c0, width, r0, r1) in enumerate(BANDS):
            n = r1 - r0
            left = jnp.concatenate([z2[0, rows, r0:r1], z2[1, rows, r0:r1]], axis=1)
            out_ref[rows, c0 : c0 + width] = dot(left, ke[ql, t, 0 : 2 * n, 0:width])

    pltpu.make_async_copy(q1.at[pl.ds(0, N_RP - 1)], q1.at[pl.ds(0, N_RP - 1)], q_send.at[0]).wait()
    pltpu.make_async_copy(q2.at[pl.ds(0, N_NEAR - 1)], q2.at[pl.ds(0, N_NEAR - 1)], q_send.at[1]).wait()
    pltpu.make_async_copy(
        q2.at[pl.ds(0, (N_FAR - 1) * N_NEAR)], q2.at[pl.ds(0, (N_FAR - 1) * N_NEAR)], q_send.at[2]
    ).wait()
    pltpu.make_async_copy(wr.at[pl.ds(0, N_RP - 1)], wr.at[pl.ds(0, N_RP - 1)], w_send.at[0]).wait()
    wait_blocks(N_DEV - 1, f_send.at[0])

    @pl.when(is_hot)
    def _():
        wait_blocks(N_DEV - 1, f_send.at[1])

    @pl.when(jnp.logical_not(is_hot))
    def _():
        pltpu.make_async_copy(wr.at[0], wr.at[0], w_send.at[1]).wait()


def local(wannier_g, rp_coords, q_coords, k_index, k_vectors, kq_vectors, modes):
    vmem = pl.BlockSpec(memory_space=pltpu.VMEM)
    smem = pl.BlockSpec(memory_space=pltpu.SMEM)
    out = pl.pallas_call(
        kernel,
        name="wannier_to_bloch",
        out_shape=jax.ShapeDtypeStruct((4 * NB, COLS), F32),
        in_specs=[pl.BlockSpec(memory_space=pl.ANY), vmem, smem, smem, vmem, vmem, vmem],
        out_specs=vmem,
        scratch_shapes=[
            pltpu.VMEM((2, R_DEV, COLS), BF16),
            pltpu.VMEM((N_RP, 2, R_DEV, LANES), BF16),
            pltpu.VMEM((N_RP, 2, R_DEV, LANES), BF16),
            pltpu.VMEM((N_RP, 4, LANES), BF16),
            pltpu.VMEM((N_PB, 4, LANES), BF16),
            pltpu.VMEM((LANES, K_ALL), BF16),
            pltpu.VMEM((N_FAR, 4 * N_RP * N_NEAR, K_ALL), BF16),
            pltpu.VMEM((N_FAR, N_RP * N_NEAR, 4, LANES), BF16),
            pltpu.VMEM((N_FAR, N_RP * N_NEAR, 4, LANES), BF16),
            pltpu.VMEM((TILES * N_PB, 4, LANES), BF16),
            pltpu.VMEM((256, LANES), BF16),
            pltpu.VMEM((2 * COLS, COLS), BF16),
            pltpu.VMEM((2, 5, 1024, 256), BF16),
            pltpu.VMEM((128, 2 * COLS), BF16),
            pltpu.VMEM((2, 128, COLS), BF16),
            pltpu.SemaphoreType.DMA,
            pltpu.SemaphoreType.DMA((3,)),
            pltpu.SemaphoreType.DMA((3,)),
            pltpu.SemaphoreType.DMA((2,)),
            pltpu.SemaphoreType.DMA((2,)),
            pltpu.SemaphoreType.DMA((2,)),
            pltpu.SemaphoreType.DMA((2,)),
        ],
        compiler_params=pltpu.CompilerParams(
            collective_id=0, has_side_effects=True, vmem_limit_bytes=60 * 2**20
        ),
    )(wannier_g[:, :, 0, :], rp_coords, q_coords.T, k_index, k_vectors, kq_vectors, modes)
    return out.reshape(2, 2, NB, COLS)


def solution(mesh):
    return jax.shard_map(
        local,
        mesh=mesh,
        in_specs=(
            P(None, "rp", "pb", None),
            P(),
            P(None, ("rp", "pb")),
            P(),
            P(),
            P(("rp", "pb"), None, None, None),
            P(("rp", "pb"), None, None, None),
        ),
        out_specs=P(("rp", "pb"), None, None, None),
        check_vma=False,
    )
```

time: 424 us -> 57.6 us (0.14)
  blocking collectives: 351 us -> 0 us
  Pallas kernels: 0 us -> 53.4 us
  waiting for transfers between devices: 20.4 us -> 0 us
  other arithmetic: 16.8 us -> 0 us
  local copies, waits for them, and re-layouts: 17 us -> 3.31 us
  starting transfers between devices: 11.5 us -> 0 us
  matrix products: 6.36 us -> 0 us
    all_gather x1 -> x0, blocking collectives: 351 us -> none  [local(): q_all = lax.all_gather(q_coords, ('rp', 'pb'), axis=1, tiled=True)]
    pallas_call x0 -> x1, Pallas kernels: none -> 53.4 us  [local(): pl.pallas_call(kernel, name='wannier_to_bloch', out_shape=jax.ShapeDtypeS...]
    all_to_all x2 -> x0, waiting for transfers between devices: 20.4 us -> none  [the longest x1 20.4 us: one_exchange(): parts = lax.all_to_all(parts, axis, split_axis=0, concat_axis=0, tiled=True)]
    all_to_all x2 -> x0, starting transfers between devices: 11.5 us -> none  [the longest x1 6.19 us: local(): lax.all_to_all(wannier_g, 'rp', split_axis=3, concat_axis=1, tiled=True)]
    neg x11 -> x0, other arithmetic: 7.81 us -> none  [the longest x8 7.76 us: phases(): -sine]
    convert_element_type x8 -> x0, other arithmetic: 7.6 us -> none  [phases(): cosine = jnp.cos(angle).astype(jnp.bfloat16)]
    dot_general x20 -> x0, matrix products: 6.36 us -> none  [the longest x8 2.35 us: fourier_block(): jnp.dot(left_imag, right, preferred_element_type=jnp.float32)]
    dynamic_update_slice x8 -> x0, local copies, waits for them, and re-layouts: 5.54 us -> none  [local(): lax.map(fourier_block, q_blocks)]
  transfers between devices with their start and end apart: 2 -> 0, of which waited for: 1 -> 0; matrix products, arithmetic and copies ran while one was open for 0% -> 0% of each run, Pallas kernels for 0% -> 0%
where the time goes in v2:
time: 57.6 us; the launch traced here: 57.3 us
  Pallas kernels  53.4 us (93%)
  local copies, waits for them, and re-layouts  3.31 us (6%)
  between operations  0.66 us (1%)
    pallas_call x1, Pallas kernels, local(): pl.pallas_call(kernel, name='wannier_to_bloch', out_shape=jax.ShapeDtypeS...  53.4 us
    unnamed x2, local copies, waits for them, and re-layouts  3.31 us

profile of v2, /device:TPU:1, one launch (start us, length us, event | category | flops | bytes accessed | tf_op | source)
XLA Modules:
  0.0 57.3 jit_solution(1307779098353133259)
XLA Ops:
  0.7 1.4 %copy.8.e_ref = bf16[2,2,36,36]{3,2,1,0:T(8,128)(2,1)} copy(bf16[2,2,36,36]{3,1,2,0:T(2,128)(2,1)} %param.13) | data formatting | bytes 20736 | tf_op args[6]
  2.0 53.4 %wannier_to_bloch.1 = f32[128,1152]{1,0:T(8,128)} custom-call(bf16[2,128,1152]{2,1,0:T(8,128)(2,1)} %bitcast.4, s32[3,1024]{1,0:T(4,128)} %rc_ref.1, s32[2,3]{1,0:T(2,128)} %bitcast.5, s32[1]{0:T(128)S(6)} %copy.10.ki_ref, bf16[8,2,32,32]{3,2,1,0:T(8,128)(2,1)} %kv_ref.1, bf16[2,2,32,32]{3,2,1,0:T(8,128)(2,1)} %kq_ref.1, bf16[2,2,36,36]{3,2,1,0:T(8,128)(2,1)} %copy.8.e_ref), custom_call_target="tpu_custom_call" | custom-call | tf_op jit(solution)/shard_map/wannier_to_bloch/pallas_call | solution.py:307
  55.4 1.9 %copy.11 = f32[2,2,32,1152]{3,2,1,0:T(8,128)} copy(f32[2,2,32,1152]{3,2,1,0:T(8,128)} %bitcast.3) | data formatting | bytes 1179648

commit v3 on v2

v3 whole, which is shorter than its diff:
```python
import functools
import math

import jax
import jax.numpy as jnp
from jax import lax
from jax.experimental import pallas as pl
from jax.experimental.pallas import tpu as pltpu
from jax.sharding import PartitionSpec as P

MESH = pl.DeviceIdType.MESH
F32 = jnp.float32
BF16 = jnp.bfloat16
NK = 16
N_RP = 8
N_PB = 32
N_FAR = 4
N_NEAR = 8
NEXT = (0, 1, 3, 2)
EARLY = 2
EARLY_ROWS = 5
SINE = (6.281640231507743, -41.11355805211909, 73.72054790475445)
ROUND = 1.5 * 2.0**23
N_DEV = N_RP * N_PB
NB = 32
NM = 36
COLS = NB * NM
R_DEV = 128
LANES = 128
TILES = COLS // LANES
NR = R_DEV * N_RP
K_ALL = 2 * R_DEV * N_RP
BANDS = tuple(
    (256 * t, min(256, COLS - 256 * t), max(0, 256 * t - 128), min(COLS, 256 * t + 384)) for t in range(5)
)


def iota(shape, dim):
    return lax.broadcasted_iota(jnp.int32, shape, dim)


def band_of(x):
    return lax.shift_right_logical(x * 1821, 16)


def dot(a, b):
    return jnp.dot(a, b, preferred_element_type=F32)


def tdot(a, b):
    return lax.dot_general(a, b, (((0,), (0,)), ((), ())), preferred_element_type=F32)


def hot_rp(pb):
    far, y_at, core = pb // 8, pb % 8 // 2, pb % 2
    even = 2 * ((y_at + far) % 4) + (y_at + far // 2) % 2
    odd = (even + 4) % 8 + 1 - 2 * (even % 2)
    return even * (1 - core) + odd * core


def onehot(cond):
    return jnp.where(cond, 1.0, 0.0).astype(BF16)


def sine(c):
    c2 = c * c
    return (c * (SINE[0] + c2 * (SINE[1] + c2 * SINE[2]))).astype(BF16)


def kernel(
    w_hbm, rc_hbm, q_ref, ki_ref, kv_hbm, kq_hbm, e_hbm, out_ref,
    wv, rc, kv, kq, em, wr, wr2, wx, wx2, q1, q2, ba, ph, send, rv, vb, ku, ke, y2, z2,
    in_sem, q_send, q_recv, w_send, w_recv, f_send, f_recv,
):
    rp, pb = lax.axis_index("rp"), lax.axis_index("pb")
    hot = hot_rp(pb)
    is_hot = rp == hot
    not_hot = rp != hot
    loads = [
        pltpu.make_async_copy(src, dst, in_sem.at[i])
        for i, (src, dst) in enumerate(((w_hbm, wv), (rc_hbm, rc), (kv_hbm, kv), (kq_hbm, kq), (e_hbm, em)))
    ]
    for load in loads:
        load.start()

    rp_peers = [lax.rem(rp + d, N_RP) for d in range(1, N_RP)]
    far, near = pb // N_NEAR, lax.rem(pb, N_NEAR)
    pb_peers = [
        (d, lax.rem(far + d, N_FAR) * N_NEAR + lax.rem(near + j, N_NEAR))
        for d in NEXT
        for j in range(1 if d == 0 else 0, N_NEAR)
    ]
    barrier = pltpu.get_barrier_semaphore()
    for other in rp_peers:
        pl.semaphore_signal(barrier, inc=1, device_id=(other, pb), device_id_type=MESH)
    for _, other in pb_peers:
        pl.semaphore_signal(barrier, inc=1, device_id=(rp, other), device_id_type=MESH)

    lane, row = iota((8, LANES), 1), iota((8, LANES), 0)
    tile = jnp.zeros((8, LANES), F32)
    for ql in range(2):
        for axis in range(3):
            tile = tile + jnp.where((lane == 16 * rp + axis) & (row == ql), q_ref[ql, axis].astype(F32), 0.0)
    q1[rp] = tile[:2].astype(BF16)

    pl.semaphore_wait(barrier, (N_RP - 1) + (N_PB - 1))

    for other in rp_peers:
        pltpu.make_async_remote_copy(
            q1.at[rp], q1.at[rp], q_send.at[0], q_recv.at[0], device_id=(other, pb), device_id_type=MESH
        ).start()
    for load in loads:
        load.wait()

    def send_w(others):
        for other in others:
            columns = pl.ds(pl.multiple_of(other * LANES, LANES), LANES)
            pltpu.make_async_remote_copy(
                wv.at[:, :, columns], wr.at[rp], w_send.at[0], w_recv.at[0], device_id=(other, pb), device_id_type=MESH
            ).start()

    send_w(rp_peers[:EARLY])

    row = iota((16, NR), 0)
    block = jnp.zeros((16, NR), F32)
    for axis in range(3):
        block = block + jnp.where(row == axis, rc[axis : axis + 1, :].astype(F32) / NK, 0.0)
    for g in range(N_RP):
        ba[16 * g : 16 * g + 16, :] = block.astype(BF16)

    wr[rp] = wv[:, :, pl.ds(pl.multiple_of(rp * LANES, LANES), LANES)]

    @pl.when(is_hot)
    def _():
        wr2[rp] = wv[:, :, pl.ds((TILES - 1) * LANES, LANES)]

    for ql in range(2):
        place = onehot(iota((NB, 2 * NB), 1) - 2 * iota((NB, 2 * NB), 0) == ql)
        for c in range(2):
            at = 64 * c + 32 * ql
            vb[at : at + 32] = tdot(kq[ql, c], place).astype(BF16)

    def band_rows(b, unit):
        spread = onehot(band_of(iota((NB, COLS), 1)) == iota((NB, COLS), 0))
        pick = onehot(band_of(b * LANES + iota((LANES, NB), 0)) == iota((LANES, NB), 1))
        r = b * LANES + iota((LANES, 1), 0)
        col = iota((1, COLS), 1)
        same = r - NM * band_of(r) == col - NM * band_of(col)
        for c in range(2):
            full = dot(dot(pick, unit[c]).astype(BF16), spread)
            ku[c * COLS + b * LANES : c * COLS + (b + 1) * LANES, :] = jnp.where(same, full, 0.0).astype(BF16)

    def branch_rows(ql):
        mode_col = iota((NM, COLS), 1)
        spread_m = onehot(mode_col - NM * band_of(mode_col) == iota((NM, COLS), 0))
        ec = dot(em[ql].reshape(2 * NM, NM), spread_m).astype(BF16)
        for t, (c0, width, r0, r1) in enumerate(BANDS):
            rows = r1 - r0
            r = r0 + iota((rows, 2 * NM), 0)
            at = iota((rows, 2 * NM), 1) - 2 * (r - NM * band_of(r))
            same = band_of(r0 + iota((rows, 1), 0)) == band_of(c0 + iota((1, width), 1))
            for c in range(2):
                full = dot(onehot(at == c), ec[:, c0 : c0 + width])
                ke[ql, t, c * rows : (c + 1) * rows, 0:width] = jnp.where(same, full, 0.0).astype(BF16)

    unit = kv[ki_ref[0]]
    for b in range(EARLY_ROWS):
        band_rows(b, unit)

    rest = q1.at[pl.ds(0, N_RP - 1)]
    pltpu.make_async_copy(rest, rest, q_recv.at[0]).wait()
    q2[pb] = jnp.sum(q1[...].astype(F32), axis=0).astype(BF16)
    for d, other in pb_peers:
        pltpu.make_async_remote_copy(
            q2.at[pb], q2.at[pb], q_send.at[1], q_recv.at[1 + (N_FAR - d) % N_FAR],
            device_id=(rp, other), device_id_type=MESH,
        ).start()
    send_w(rp_peers[EARLY:])

    @pl.when(not_hot)
    def _():
        last = wv.at[:, :, pl.ds((TILES - 1) * LANES, LANES)]
        pltpu.make_async_remote_copy(
            last, wr2.at[rp], w_send.at[1], w_recv.at[1], device_id=(hot, pb), device_id_type=MESH
        ).start()

    def fill_phases(d):
        rest = q2.at[pl.ds(0, N_NEAR - (d == 0))]
        pltpu.make_async_copy(rest, rest, q_recv.at[1 + d]).wait()
        z = lax.rem(far + d, N_FAR)
        some = q2[pl.ds(z * N_NEAR, N_NEAR)].astype(F32).reshape(2 * N_NEAR, LANES)
        group = iota((2 * N_NEAR, LANES), 1) // 16
        left = jnp.concatenate([jnp.where(group == g, some, 0.0) for g in range(N_RP)], axis=0).astype(BF16)
        for p in range(N_RP):
            turns = dot(left, ba[:, p * R_DEV : (p + 1) * R_DEV])
            y = turns - ((turns + ROUND) - ROUND)
            at = 2 * p * LANES
            ph[z, :, at : at + LANES] = sine(0.25 - jnp.abs(y))
            ph[z, :, at + LANES : at + 2 * LANES] = sine(jnp.maximum(jnp.minimum(y, 0.5 - y), -0.5 - y))

    for b in range(EARLY_ROWS, 9):
        band_rows(b, unit)
    branch_rows(0)
    fill_phases(0)
    branch_rows(1)
    fill_phases(1)
    fill_phases(3)
    fill_phases(2)

    rest = wr.at[pl.ds(0, N_RP - 1)]
    pltpu.make_async_copy(rest, rest, w_recv.at[0]).wait()

    def both_parts(src, dst):
        for p in range(N_RP):
            re, im = src[p, 0], src[p, 1]
            dst[256 * p : 256 * p + 128, 0:128] = re
            dst[256 * p : 256 * p + 128, 128:256] = im
            dst[256 * p + 128 : 256 * p + 256, 0:128] = -im
            dst[256 * p + 128 : 256 * p + 256, 128:256] = re

    both_parts(wr, wx)

    @pl.when(is_hot)
    def _():
        rest = wr2.at[pl.ds(0, N_RP - 1)]
        pltpu.make_async_copy(rest, rest, w_recv.at[1]).wait()
        both_parts(wr2, wx2)

    me = rp * N_PB + pb

    mine = rp * N_NEAR + near

    def blocks_to(src, dst, sem, z, g):
        to_rp = lax.rem(rp + g, N_RP)

        def push(j):
            to_near = lax.rem(near + j, N_NEAR)
            pltpu.make_async_remote_copy(
                src(to_rp * N_NEAR + to_near), dst, f_send.at[sem], f_recv.at[sem],
                device_id=(to_rp, z * N_NEAR + to_near), device_id_type=MESH,
            ).start()

        @pl.when((to_rp != rp) | (z != far))
        def _():
            push(0)

        for j in range(1, N_NEAR):
            push(j)

    for d in NEXT:
        z = lax.rem(far + d, N_FAR)
        send[z, :, 0] = dot(ph[z], wx[...]).astype(BF16).reshape(64, 2, 256)

        @pl.when(is_hot)
        def _():
            send[z, :, 1] = dot(ph[z], wx2[...]).astype(BF16).reshape(64, 2, 256)

            @pl.loop(0, N_RP // 2)
            def _(g):
                for i in range(2):
                    blocks_to(lambda at: send.at[z, at], rv.at[me], 1, z, 2 * g + i)

        @pl.when(not_hot)
        def _():
            @pl.loop(0, N_RP // 2)
            def _(g):
                for i in range(2):
                    blocks_to(lambda at: send.at[z, at, 0], rv.at[me, 0], 0, z, 2 * g + i)

    rv[me, 0] = send[far, mine, 0]

    @pl.when(is_hot)
    def _():
        rv[me, 1] = send[far, mine, 1]

    def wait_pairs(count, sem):
        rest = rv.at[pl.ds(0, count)]
        pltpu.make_async_copy(rest, rest, sem).wait()

    def wait_blocks(count, sem):
        rest = rv.at[pl.ds(0, count), 0]
        pltpu.make_async_copy(rest, rest, sem).wait()

    @pl.when(is_hot)
    def _():
        wait_pairs(N_PB - 1, f_recv.at[1])
        wait_blocks(N_DEV - N_PB, f_recv.at[0])

    @pl.when(not_hot)
    def _():
        wait_pairs(N_PB, f_recv.at[1])
        wait_blocks(N_DEV - N_PB - 1, f_recv.at[0])

    for t in range(TILES):
        if t < N_RP:
            got = rv[t * N_PB : (t + 1) * N_PB, 0].reshape(2 * N_PB, 256)
        else:
            got = jnp.concatenate([rv[hot_rp(m) * N_PB + m : hot_rp(m) * N_PB + m + 1, 1] for m in range(N_PB)], axis=0)
            got = got.reshape(2 * N_PB, 256)
        part = dot(vb[...], got)
        re = (part[:64, :128] + part[64:, 128:]).astype(BF16)
        im = part[:64, 128:] - part[64:, :128]
        cols = slice(t * LANES, (t + 1) * LANES)
        more = slice(COLS + t * LANES, COLS + (t + 1) * LANES)
        y2[:64, cols] = re
        y2[64:, cols] = im.astype(BF16)
        y2[:64, more] = (-im).astype(BF16)
        y2[64:, more] = re
    for c0, width, _, _ in BANDS:
        part = dot(y2[...], ku[:, c0 : c0 + width])
        cols = slice(c0, c0 + width)
        for ql in range(2):
            re, im = part[32 * ql : 32 * ql + 32], part[64 + 32 * ql : 96 + 32 * ql]
            at = 64 * ql
            z2[0, at : at + 32, cols] = re.astype(BF16)
            z2[0, at + 32 : at + 64, cols] = im.astype(BF16)
            z2[1, at : at + 32, cols] = (-im).astype(BF16)
            z2[1, at + 32 : at + 64, cols] = re.astype(BF16)
    for ql in range(2):
        rows = slice(64 * ql, 64 * ql + 64)
        for t, (c0, width, r0, r1) in enumerate(BANDS):
            n = r1 - r0
            left = jnp.concatenate([z2[0, rows, r0:r1], z2[1, rows, r0:r1]], axis=1)
            out_ref[rows, c0 : c0 + width] = dot(left, ke[ql, t, 0 : 2 * n, 0:width])

    rest = q1.at[pl.ds(0, N_RP - 1)]
    pltpu.make_async_copy(rest, rest, q_send.at[0]).wait()
    rest = q2.at[pl.ds(0, N_PB - 1)]
    pltpu.make_async_copy(rest, rest, q_send.at[1]).wait()
    rest = wr.at[pl.ds(0, N_RP - 1)]
    pltpu.make_async_copy(rest, rest, w_send.at[0]).wait()

    @pl.when(is_hot)
    def _():
        wait_pairs(N_DEV - 1, f_send.at[1])

    @pl.when(not_hot)
    def _():
        wait_blocks(N_DEV - 1, f_send.at[0])
        pltpu.make_async_copy(wr.at[0], wr.at[0], w_send.at[1]).wait()


def local(wannier_g, rp_coords, q_coords, k_index, k_vectors, kq_vectors, modes):
    vmem = pl.BlockSpec(memory_space=pltpu.VMEM)
    smem = pl.BlockSpec(memory_space=pltpu.SMEM)
    hbm = pl.BlockSpec(memory_space=pltpu.HBM)
    out = pl.pallas_call(
        kernel,
        name="wannier_to_bloch",
        out_shape=pltpu.VMEM((4 * NB, COLS), F32),
        in_specs=[hbm, hbm, smem, smem, hbm, hbm, hbm],
        out_specs=vmem,
        scratch_shapes=[
            pltpu.VMEM((2, R_DEV, COLS), BF16),
            pltpu.VMEM((3, NR), jnp.int32),
            pltpu.VMEM(k_vectors.shape, BF16),
            pltpu.VMEM(kq_vectors.shape, BF16),
            pltpu.VMEM((2, NM, 2, NM), BF16),
            pltpu.VMEM((N_RP, 2, R_DEV, LANES), BF16),
            pltpu.VMEM((N_RP, 2, R_DEV, LANES), BF16),
            pltpu.VMEM((K_ALL, 256), BF16),
            pltpu.VMEM((K_ALL, 256), BF16),
            pltpu.VMEM((N_RP, 2, LANES), BF16),
            pltpu.VMEM((N_PB, 2, LANES), BF16),
            pltpu.VMEM((LANES, NR), BF16),
            pltpu.VMEM((N_FAR, 2 * N_RP * N_NEAR, K_ALL), BF16),
            pltpu.VMEM((N_FAR, N_RP * N_NEAR, 2, 2, 256), BF16),
            pltpu.VMEM((N_DEV, 2, 2, 256), BF16),
            pltpu.VMEM((128, 64), BF16),
            pltpu.VMEM((2 * COLS, COLS), BF16),
            pltpu.VMEM((2, 5, 1024, 256), BF16),
            pltpu.VMEM((128, 2 * COLS), BF16),
            pltpu.VMEM((2, 128, COLS), BF16),
            pltpu.SemaphoreType.DMA((5,)),
            pltpu.SemaphoreType.DMA((2,)),
            pltpu.SemaphoreType.DMA((5,)),
            pltpu.SemaphoreType.DMA((2,)),
            pltpu.SemaphoreType.DMA((2,)),
            pltpu.SemaphoreType.DMA((2,)),
            pltpu.SemaphoreType.DMA((2,)),
        ],
        compiler_params=pltpu.CompilerParams(
            collective_id=0, has_side_effects=True, vmem_limit_bytes=58 * 2**20
        ),
    )(wannier_g[:, :, 0, :], rp_coords, q_coords.T, k_index, k_vectors, kq_vectors, modes.transpose(0, 2, 1, 3))
    return out.reshape(2, 2, NB, COLS)


def solution(mesh):
    return jax.shard_map(
        local,
        mesh=mesh,
        in_specs=(
            P(None, "rp", "pb", None),
            P(),
            P(None, ("rp", "pb")),
            P(),
            P(),
            P(("rp", "pb"), None, None, None),
            P(("rp", "pb"), None, None, None),
        ),
        out_specs=P(("rp", "pb"), None, None, None),
        check_vma=False,
    )
```

time: 57.6 us -> 41.6 us (0.72)
  Pallas kernels: 53.4 us -> 40 us
  local copies, waits for them, and re-layouts: 3.31 us -> 0.82 us
    pallas_call x1, Pallas kernels: 53.4 us -> 40 us  [local(): pl.pallas_call(kernel, name='wannier_to_bloch', out_shape=pltpu.VMEM((4 *...]
    unnamed x2 -> x1, local copies, waits for them, and re-layouts: 3.31 us -> 0.82 us
where the time goes in v3:
time: 41.6 us; the launch traced here: 41.5 us
  Pallas kernels  40 us (96%)
  local copies, waits for them, and re-layouts  0.82 us (2%)
  between operations  0.66 us (2%)
    pallas_call x1, Pallas kernels, local(): pl.pallas_call(kernel, name='wannier_to_bloch', out_shape=pltpu.VMEM((4 *...  40 us

profile of v3, /device:TPU:1, one launch (start us, length us, event | category | flops | bytes accessed | tf_op | source)
XLA Modules:
  0.0 41.5 jit_solution(8728558939104629805)
XLA Ops:
  0.7 40.0 %wannier_to_bloch.1 = f32[128,1152]{1,0:T(8,128)S(1)} custom-call(bf16[2,128,1152]{2,1,0:T(8,128)(2,1)} %bitcast.5, s32[3,1024]{1,0:T(4,128)} %rc_hbm.1, s32[2,3]{1,0:T(2,128)} %bitcast.7, s32[1]{0:T(128)S(6)} %copy.10.ki_ref, bf16[8,2,32,32]{3,2,1,0:T(8,128)(2,1)} %kv_hbm.1, bf16[2,2,32,32]{3,2,1,0:T(8,128)(2,1)} %kq_hbm.1, bf16[2,36,2,36]{3,2,1,0:T(2,128)(2,1)} %bitcast.6), custom_call_target="tpu_custom_call" | custom-call | tf_op jit(solution)/shard_map/wannier_to_bloch/pallas_call | solution.py:347
  40.6 0.8 %copy.9 = f32[2,2,32,1152]{3,2,1,0:T(8,128)} copy(f32[2,2,32,1152]{3,2,1,0:T(8,128)S(1)} %bitcast.4) | data formatting | bytes 1179648

commit v4 on v3

--- a/solution.py
+++ b/solution.py
@@ -17,8 +17,10 @@
 N_FAR = 4
 N_NEAR = 8
 NEXT = (0, 1, 3, 2)
-EARLY = 2
-EARLY_ROWS = 5
+EARLY = ((1, 0), (0, 1), (3, 0), (1, 1), (3, 1))
+LATE = ((2, 1), (2, 0))
+ORDER = (2, 1, 3, 0)
+EARLY_ROWS = 6
 SINE = (6.281640231507743, -41.11355805211909, 73.72054790475445)
 ROUND = 1.5 * 2.0**23
 N_DEV = N_RP * N_PB
@@ -68,8 +70,8 @@
 
 
 def kernel(
-    w_hbm, rc_hbm, q_ref, ki_ref, kv_hbm, kq_hbm, e_hbm, out_ref,
-    wv, rc, kv, kq, em, wr, wr2, wx, wx2, q1, q2, ba, ph, send, rv, vb, ku, ke, y2, z2,
+    w_hbm, rc_hbm, q_hbm, ki_hbm, kv_hbm, kq_hbm, e_hbm, out_ref,
+    wv, rc, q_ref, ki_ref, kv, kq, em, wr, wr2, wx, wx2, q1, q2, ba, ph, send, rv, vb, ku, ke, y2, z2,
     in_sem, q_send, q_recv, w_send, w_recv, f_send, f_recv,
 ):
     rp, pb = lax.axis_index("rp"), lax.axis_index("pb")
@@ -78,54 +80,85 @@
     not_hot = rp != hot
     loads = [
         pltpu.make_async_copy(src, dst, in_sem.at[i])
-        for i, (src, dst) in enumerate(((w_hbm, wv), (rc_hbm, rc), (kv_hbm, kv), (kq_hbm, kq), (e_hbm, em)))
+        for i, (src, dst) in enumerate(
+            (
+                (q_hbm, q_ref),
+                (ki_hbm, ki_ref),
+                (w_hbm, wv),
+                (rc_hbm, rc),
+                (kv_hbm, kv),
+                (kq_hbm, kq),
+                (e_hbm, em),
+            )
+        )
     ]
     for load in loads:
         load.start()
 
-    rp_peers = [lax.rem(rp + d, N_RP) for d in range(1, N_RP)]
+    def w_peer(step):
+        z = lax.rem(rp, 2)
+        return 2 * lax.rem(rp // 2 + step[0], 4) + z + step[1] - 2 * z * step[1]
+
     far, near = pb // N_NEAR, lax.rem(pb, N_NEAR)
-    pb_peers = [
-        (d, lax.rem(far + d, N_FAR) * N_NEAR + lax.rem(near + j, N_NEAR))
-        for d in NEXT
-        for j in range(1 if d == 0 else 0, N_NEAR)
+    x, z = rp // 2, lax.rem(rp, 2)
+    flip = 1 - 2 * z
+    flat_peers = [
+        (2 * lax.rem(x + i, 4) + z, far * N_NEAR + lax.rem(near + j, N_NEAR))
+        for i in range(4)
+        for j in range(N_NEAR)
+        if i + j
     ]
+    deep_peers = [
+        (d, (rp + f * flip, lax.rem(far + d, N_FAR) * N_NEAR + near)) for d in NEXT for f in range(2) if d + f
+    ]
+    other_peers = [(2 * lax.rem(x + i, 4) + z + flip, pb) for i in range(1, 4)]
     barrier = pltpu.get_barrier_semaphore()
-    for other in rp_peers:
-        pl.semaphore_signal(barrier, inc=1, device_id=(other, pb), device_id_type=MESH)
-    for _, other in pb_peers:
-        pl.semaphore_signal(barrier, inc=1, device_id=(rp, other), device_id_type=MESH)
-
+    for other in flat_peers + [other for _, other in deep_peers] + other_peers:
+        pl.semaphore_signal(barrier, inc=1, device_id=other, device_id_type=MESH)
+
+    loads[0].wait()
+    flat = x * N_NEAR + near
     lane, row = iota((8, LANES), 1), iota((8, LANES), 0)
     tile = jnp.zeros((8, LANES), F32)
     for ql in range(2):
         for axis in range(3):
-            tile = tile + jnp.where((lane == 16 * rp + axis) & (row == ql), q_ref[ql, axis].astype(F32), 0.0)
-    q1[rp] = tile[:2].astype(BF16)
-
-    pl.semaphore_wait(barrier, (N_RP - 1) + (N_PB - 1))
-
-    for other in rp_peers:
+            tile = tile + jnp.where((lane == 4 * flat + axis) & (row == ql), q_ref[ql, axis].astype(F32), 0.0)
+    q1[flat] = tile[:2].astype(BF16)
+
+    pl.semaphore_wait(barrier, len(flat_peers) + len(deep_peers) + len(other_peers))
+
+    for other in flat_peers:
         pltpu.make_async_remote_copy(
-            q1.at[rp], q1.at[rp], q_send.at[0], q_recv.at[0], device_id=(other, pb), device_id_type=MESH
+            q1.at[flat], q1.at[flat], q_send.at[0], q_recv.at[0], device_id=other, device_id_type=MESH
         ).start()
-    for load in loads:
+    for load in loads[1:]:
         load.wait()
 
-    def send_w(others):
-        for other in others:
+    def send_last():
+        last = wv.at[:, :, pl.ds((TILES - 1) * LANES, LANES)]
+        pltpu.make_async_remote_copy(
+            last, wr2.at[rp], w_send.at[1], w_recv.at[1], device_id=(hot, pb), device_id_type=MESH
+        ).start()
+
+    def send_w(steps):
+        for step in steps:
+            other = 2 * lax.rem(x + step[0], 4) + z + step[1] * flip
             columns = pl.ds(pl.multiple_of(other * LANES, LANES), LANES)
             pltpu.make_async_remote_copy(
                 wv.at[:, :, columns], wr.at[rp], w_send.at[0], w_recv.at[0], device_id=(other, pb), device_id_type=MESH
             ).start()
 
-    send_w(rp_peers[:EARLY])
-
-    row = iota((16, NR), 0)
+    @pl.when(not_hot)
+    def _():
+        send_last()
+
+    send_w(EARLY)
+
+    row = iota((16, NR), 0) % 4
     block = jnp.zeros((16, NR), F32)
     for axis in range(3):
         block = block + jnp.where(row == axis, rc[axis : axis + 1, :].astype(F32) / NK, 0.0)
-    for g in range(N_RP):
+    for g in range(LANES // 16):
         ba[16 * g : 16 * g + 16, :] = block.astype(BF16)
 
     wr[rp] = wv[:, :, pl.ds(pl.multiple_of(rp * LANES, LANES), LANES)]
@@ -167,42 +200,34 @@
     for b in range(EARLY_ROWS):
         band_rows(b, unit)
 
-    rest = q1.at[pl.ds(0, N_RP - 1)]
+    rest = q1.at[pl.ds(0, len(flat_peers))]
     pltpu.make_async_copy(rest, rest, q_recv.at[0]).wait()
-    q2[pb] = jnp.sum(q1[...].astype(F32), axis=0).astype(BF16)
-    for d, other in pb_peers:
+    deep = 2 * far + z
+    q2[deep] = jnp.sum(q1[...].astype(F32), axis=0).astype(BF16)
+    for d, other in deep_peers:
         pltpu.make_async_remote_copy(
-            q2.at[pb], q2.at[pb], q_send.at[1], q_recv.at[1 + (N_FAR - d) % N_FAR],
-            device_id=(rp, other), device_id_type=MESH,
+            q2.at[deep], q2.at[deep], q_send.at[1], q_recv.at[1 + (N_FAR - d) % N_FAR],
+            device_id=other, device_id_type=MESH,
         ).start()
-    send_w(rp_peers[EARLY:])
-
-    @pl.when(not_hot)
-    def _():
-        last = wv.at[:, :, pl.ds((TILES - 1) * LANES, LANES)]
-        pltpu.make_async_remote_copy(
-            last, wr2.at[rp], w_send.at[1], w_recv.at[1], device_id=(hot, pb), device_id_type=MESH
-        ).start()
+    send_w(LATE)
 
     def fill_phases(d):
-        rest = q2.at[pl.ds(0, N_NEAR - (d == 0))]
+        rest = q2.at[pl.ds(0, 2 - (d == 0))]
         pltpu.make_async_copy(rest, rest, q_recv.at[1 + d]).wait()
-        z = lax.rem(far + d, N_FAR)
-        some = q2[pl.ds(z * N_NEAR, N_NEAR)].astype(F32).reshape(2 * N_NEAR, LANES)
-        group = iota((2 * N_NEAR, LANES), 1) // 16
-        left = jnp.concatenate([jnp.where(group == g, some, 0.0) for g in range(N_RP)], axis=0).astype(BF16)
+        group = lax.rem(far + d, N_FAR)
+        row, lane = iota((LANES, LANES), 0), iota((LANES, LANES), 1)
+        some = [q2[2 * group + i].astype(F32) for i in range(2)]
+        row_of = [jnp.where(row % 2 == 0, some[i][0:1], some[i][1:2]) for i in range(2)]
+        own = lane // 4 == row // 32 * N_NEAR + row // 2 % N_NEAR
+        left = jnp.where(own, jnp.where(row // 16 % 2 == 0, row_of[0], row_of[1]), 0.0).astype(BF16)
         for p in range(N_RP):
             turns = dot(left, ba[:, p * R_DEV : (p + 1) * R_DEV])
             y = turns - ((turns + ROUND) - ROUND)
             at = 2 * p * LANES
-            ph[z, :, at : at + LANES] = sine(0.25 - jnp.abs(y))
-            ph[z, :, at + LANES : at + 2 * LANES] = sine(jnp.maximum(jnp.minimum(y, 0.5 - y), -0.5 - y))
-
-    for b in range(EARLY_ROWS, 9):
-        band_rows(b, unit)
-    branch_rows(0)
+            ph[group, :, at : at + LANES] = sine(0.25 - jnp.abs(y))
+            ph[group, :, at + LANES : at + 2 * LANES] = sine(jnp.maximum(jnp.minimum(y, 0.5 - y), -0.5 - y))
+
     fill_phases(0)
-    branch_rows(1)
     fill_phases(1)
     fill_phases(3)
     fill_phases(2)
@@ -230,48 +255,53 @@
 
     mine = rp * N_NEAR + near
 
-    def blocks_to(src, dst, sem, z, g):
+    def blocks_to(src, dst, sem, group, g):
         to_rp = lax.rem(rp + g, N_RP)
 
         def push(j):
             to_near = lax.rem(near + j, N_NEAR)
             pltpu.make_async_remote_copy(
                 src(to_rp * N_NEAR + to_near), dst, f_send.at[sem], f_recv.at[sem],
-                device_id=(to_rp, z * N_NEAR + to_near), device_id_type=MESH,
+                device_id=(to_rp, group * N_NEAR + to_near), device_id_type=MESH,
             ).start()
 
-        @pl.when((to_rp != rp) | (z != far))
+        @pl.when((to_rp != rp) | (group != far))
         def _():
             push(0)
 
         for j in range(1, N_NEAR):
             push(j)
 
-    for d in NEXT:
-        z = lax.rem(far + d, N_FAR)
-        send[z, :, 0] = dot(ph[z], wx[...]).astype(BF16).reshape(64, 2, 256)
+    for d in ORDER:
+        group = lax.rem(far + d, N_FAR)
+        send[group, :, 0] = dot(ph[group], wx[...]).astype(BF16).reshape(64, 2, 256)
 
         @pl.when(is_hot)
         def _():
-            send[z, :, 1] = dot(ph[z], wx2[...]).astype(BF16).reshape(64, 2, 256)
+            send[group, :, 1] = dot(ph[group], wx2[...]).astype(BF16).reshape(64, 2, 256)
 
             @pl.loop(0, N_RP // 2)
             def _(g):
                 for i in range(2):
-                    blocks_to(lambda at: send.at[z, at], rv.at[me], 1, z, 2 * g + i)
+                    blocks_to(lambda at: send.at[group, at], rv.at[me], 1, group, 2 * g + i)
 
         @pl.when(not_hot)
         def _():
             @pl.loop(0, N_RP // 2)
             def _(g):
                 for i in range(2):
-                    blocks_to(lambda at: send.at[z, at, 0], rv.at[me, 0], 0, z, 2 * g + i)
+                    blocks_to(lambda at: send.at[group, at, 0], rv.at[me, 0], 0, group, 2 * g + i)
 
     rv[me, 0] = send[far, mine, 0]
 
     @pl.when(is_hot)
     def _():
         rv[me, 1] = send[far, mine, 1]
+
+    for b in range(EARLY_ROWS, 9):
+        band_rows(b, unit)
+    branch_rows(0)
+    branch_rows(1)
 
     def wait_pairs(count, sem):
         rest = rv.at[pl.ds(0, count)]
@@ -323,9 +353,9 @@
             left = jnp.concatenate([z2[0, rows, r0:r1], z2[1, rows, r0:r1]], axis=1)
             out_ref[rows, c0 : c0 + width] = dot(left, ke[ql, t, 0 : 2 * n, 0:width])
 
-    rest = q1.at[pl.ds(0, N_RP - 1)]
+    rest = q1.at[pl.ds(0, len(flat_peers))]
     pltpu.make_async_copy(rest, rest, q_send.at[0]).wait()
-    rest = q2.at[pl.ds(0, N_PB - 1)]
+    rest = q2.at[pl.ds(0, len(deep_peers))]
     pltpu.make_async_copy(rest, rest, q_send.at[1]).wait()
     rest = wr.at[pl.ds(0, N_RP - 1)]
     pltpu.make_async_copy(rest, rest, w_send.at[0]).wait()
@@ -342,17 +372,18 @@
 
 def local(wannier_g, rp_coords, q_coords, k_index, k_vectors, kq_vectors, modes):
     vmem = pl.BlockSpec(memory_space=pltpu.VMEM)
-    smem = pl.BlockSpec(memory_space=pltpu.SMEM)
     hbm = pl.BlockSpec(memory_space=pltpu.HBM)
     out = pl.pallas_call(
         kernel,
         name="wannier_to_bloch",
         out_shape=pltpu.VMEM((4 * NB, COLS), F32),
-        in_specs=[hbm, hbm, smem, smem, hbm, hbm, hbm],
+        in_specs=[hbm] * 7,
         out_specs=vmem,
         scratch_shapes=[
             pltpu.VMEM((2, R_DEV, COLS), BF16),
             pltpu.VMEM((3, NR), jnp.int32),
+            pltpu.SMEM((2, 3), jnp.int32),
+            pltpu.SMEM((1,), jnp.int32),
             pltpu.VMEM(k_vectors.shape, BF16),
             pltpu.VMEM(kq_vectors.shape, BF16),
             pltpu.VMEM((2, NM, 2, NM), BF16),
@@ -360,8 +391,8 @@
             pltpu.VMEM((N_RP, 2, R_DEV, LANES), BF16),
             pltpu.VMEM((K_ALL, 256), BF16),
             pltpu.VMEM((K_ALL, 256), BF16),
-            pltpu.VMEM((N_RP, 2, LANES), BF16),
             pltpu.VMEM((N_PB, 2, LANES), BF16),
+            pltpu.VMEM((2 * N_FAR, 2, LANES), BF16),
             pltpu.VMEM((LANES, NR), BF16),
             pltpu.VMEM((N_FAR, 2 * N_RP * N_NEAR, K_ALL), BF16),
             pltpu.VMEM((N_FAR, N_RP * N_NEAR, 2, 2, 256), BF16),
@@ -371,7 +402,7 @@
             pltpu.VMEM((2, 5, 1024, 256), BF16),
             pltpu.VMEM((128, 2 * COLS), BF16),
             pltpu.VMEM((2, 128, COLS), BF16),
-            pltpu.SemaphoreType.DMA((5,)),
+            pltpu.SemaphoreType.DMA((7,)),
             pltpu.SemaphoreType.DMA((2,)),
             pltpu.SemaphoreType.DMA((5,)),
             pltpu.SemaphoreType.DMA((2,)),

time: 41.6 us -> 36.7 us (0.88)
  Pallas kernels: 40 us -> 35.1 us
    pallas_call x1, Pallas kernels: 40 us -> 35.1 us  [local(): pl.pallas_call(kernel, name='wannier_to_bloch', out_shape=pltpu.VMEM((4 *...]
where the time goes in v4:
time: 36.7 us; the launch traced here: 36.6 us
  Pallas kernels  35.1 us (96%)
  local copies, waits for them, and re-layouts  0.82 us (2%)
  between operations  0.66 us (2%)
    pallas_call x1, Pallas kernels, local(): pl.pallas_call(kernel, name='wannier_to_bloch', out_shape=pltpu.VMEM((4 *...  35.1 us
    unnamed x1, local copies, waits for them, and re-layouts  0.82 us

profile of v4, /device:TPU:1, one launch (start us, length us, event | category | flops | bytes accessed | tf_op | source)
XLA Modules:
  0.0 36.6 jit_solution(8331092479219326077)
XLA Ops:
  0.7 35.1 %wannier_to_bloch.1 = f32[128,1152]{1,0:T(8,128)S(1)} custom-call(bf16[2,128,1152]{2,1,0:T(8,128)(2,1)} %bitcast.5, s32[3,1024]{1,0:T(4,128)} %rc_hbm.1, s32[2,3]{1,0:T(2,128)} %bitcast.7, s32[1]{0:T(128)S(6)} %copy.10.ki_hbm, bf16[8,2,32,32]{3,2,1,0:T(8,128)(2,1)} %kv_hbm.1, bf16[2,2,32,32]{3,2,1,0:T(8,128)(2,1)} %kq_hbm.1, bf16[2,36,2,36]{3,2,1,0:T(2,128)(2,1)} %bitcast.6), custom_call_target="tpu_custom_call" | custom-call | tf_op jit(solution)/shard_map/wannier_to_bloch/pallas_call | solution.py:376
  35.8 0.8 %copy.9 = f32[2,2,32,1152]{3,2,1,0:T(8,128)} copy(f32[2,2,32,1152]{3,2,1,0:T(8,128)S(1)} %bitcast.4) | data formatting | bytes 1179648

commit v5 on v4

--- a/solution.py
+++ b/solution.py
@@ -16,10 +16,9 @@
 N_PB = 32
 N_FAR = 4
 N_NEAR = 8
-NEXT = (0, 1, 3, 2)
+NEXT = (2, 1, 3, 0)
 EARLY = ((1, 0), (0, 1), (3, 0), (1, 1), (3, 1))
 LATE = ((2, 1), (2, 0))
-ORDER = (2, 1, 3, 0)
 EARLY_ROWS = 6
 SINE = (6.281640231507743, -41.11355805211909, 73.72054790475445)
 ROUND = 1.5 * 2.0**23
@@ -71,7 +70,7 @@
 
 def kernel(
     w_hbm, rc_hbm, q_hbm, ki_hbm, kv_hbm, kq_hbm, e_hbm, out_ref,
-    wv, rc, q_ref, ki_ref, kv, kq, em, wr, wr2, wx, wx2, q1, q2, ba, ph, send, rv, vb, ku, ke, y2, z2,
+    wv, rc, q_ref, ki_ref, kv, kq, em, wr, wr2, wx, q1, q2, ba, ph, send, rv, vb, ku, ke, y2, z2,
     in_sem, q_send, q_recv, w_send, w_recv, f_send, f_recv,
 ):
     rp, pb = lax.axis_index("rp"), lax.axis_index("pb")
@@ -104,8 +103,8 @@
     flip = 1 - 2 * z
     flat_peers = [
         (2 * lax.rem(x + i, 4) + z, far * N_NEAR + lax.rem(near + j, N_NEAR))
-        for i in range(4)
-        for j in range(N_NEAR)
+        for i in (2, 1, 3, 0)
+        for j in (4, 5, 2, 3, 6, 7, 1, 0)
         if i + j
     ]
     deep_peers = [
@@ -113,7 +112,7 @@
     ]
     other_peers = [(2 * lax.rem(x + i, 4) + z + flip, pb) for i in range(1, 4)]
     barrier = pltpu.get_barrier_semaphore()
-    for other in flat_peers + [other for _, other in deep_peers] + other_peers:
+    for other in [other for _, other in deep_peers] + flat_peers + other_peers:
         pl.semaphore_signal(barrier, inc=1, device_id=other, device_id_type=MESH)
 
     loads[0].wait()
@@ -235,21 +234,21 @@
     rest = wr.at[pl.ds(0, N_RP - 1)]
     pltpu.make_async_copy(rest, rest, w_recv.at[0]).wait()
 
-    def both_parts(src, dst):
+    def both_parts(src, at):
         for p in range(N_RP):
             re, im = src[p, 0], src[p, 1]
-            dst[256 * p : 256 * p + 128, 0:128] = re
-            dst[256 * p : 256 * p + 128, 128:256] = im
-            dst[256 * p + 128 : 256 * p + 256, 0:128] = -im
-            dst[256 * p + 128 : 256 * p + 256, 128:256] = re
-
-    both_parts(wr, wx)
+            wx[256 * p : 256 * p + 128, at : at + 128] = re
+            wx[256 * p : 256 * p + 128, at + 128 : at + 256] = im
+            wx[256 * p + 128 : 256 * p + 256, at : at + 128] = -im
+            wx[256 * p + 128 : 256 * p + 256, at + 128 : at + 256] = re
+
+    both_parts(wr, 0)
 
     @pl.when(is_hot)
     def _():
         rest = wr2.at[pl.ds(0, N_RP - 1)]
         pltpu.make_async_copy(rest, rest, w_recv.at[1]).wait()
-        both_parts(wr2, wx2)
+        both_parts(wr2, 256)
 
     me = rp * N_PB + pb
 
@@ -272,13 +271,13 @@
         for j in range(1, N_NEAR):
             push(j)
 
-    for d in ORDER:
+    for d in (2, 1 + 2 * z, 3 - 2 * z, 0):
         group = lax.rem(far + d, N_FAR)
-        send[group, :, 0] = dot(ph[group], wx[...]).astype(BF16).reshape(64, 2, 256)
-
         @pl.when(is_hot)
         def _():
-            send[group, :, 1] = dot(ph[group], wx2[...]).astype(BF16).reshape(64, 2, 256)
+            part = dot(ph[group], wx[...]).astype(BF16)
+            for slot in range(2):
+                send[group, :, slot] = part[:, 256 * slot : 256 * slot + 256].reshape(64, 2, 256)
 
             @pl.loop(0, N_RP // 2)
             def _(g):
@@ -287,6 +286,8 @@
 
         @pl.when(not_hot)
         def _():
+            send[group, :, 0] = dot(ph[group], wx[:, 0:256]).astype(BF16).reshape(64, 2, 256)
+
             @pl.loop(0, N_RP // 2)
             def _(g):
                 for i in range(2):
@@ -389,8 +390,7 @@
             pltpu.VMEM((2, NM, 2, NM), BF16),
             pltpu.VMEM((N_RP, 2, R_DEV, LANES), BF16),
             pltpu.VMEM((N_RP, 2, R_DEV, LANES), BF16),
-            pltpu.VMEM((K_ALL, 256), BF16),
-            pltpu.VMEM((K_ALL, 256), BF16),
+            pltpu.VMEM((K_ALL, 512), BF16),
             pltpu.VMEM((N_PB, 2, LANES), BF16),
             pltpu.VMEM((2 * N_FAR, 2, LANES), BF16),
             pltpu.VMEM((LANES, NR), BF16),

time: 36.7 us -> 36 us (0.981)
  Pallas kernels: 35.1 us -> 34.5 us
    pallas_call x1, Pallas kernels: 35.1 us -> 34.5 us  [local(): pl.pallas_call(kernel, name='wannier_to_bloch', out_shape=pltpu.VMEM((4 *...]
where the time goes in v5:
time: 36 us
  Pallas kernels  34.5 us (96%)
  local copies, waits for them, and re-layouts  0.82 us (2%)
  between operations  0.66 us (2%)
    pallas_call x1, Pallas kernels, local(): pl.pallas_call(kernel, name='wannier_to_bloch', out_shape=pltpu.VMEM((4 *...  34.5 us
    unnamed x1, local copies, waits for them, and re-layouts  0.82 us

profile of v5, /device:TPU:1, one launch (start us, length us, event | category | flops | bytes accessed | tf_op | source)
XLA Modules:
  0.0 36.0 jit_solution(16341067363765524618)
XLA Ops:
  0.7 34.5 %wannier_to_bloch.1 = f32[128,1152]{1,0:T(8,128)S(1)} custom-call(bf16[2,128,1152]{2,1,0:T(8,128)(2,1)} %bitcast.5, s32[3,1024]{1,0:T(4,128)} %rc_hbm.1, s32[2,3]{1,0:T(2,128)} %bitcast.7, s32[1]{0:T(128)S(6)} %copy.10.ki_hbm, bf16[8,2,32,32]{3,2,1,0:T(8,128)(2,1)} %kv_hbm.1, bf16[2,2,32,32]{3,2,1,0:T(8,128)(2,1)} %kq_hbm.1, bf16[2,36,2,36]{3,2,1,0:T(2,128)(2,1)} %bitcast.6), custom_call_target="tpu_custom_call" | custom-call | tf_op jit(solution)/shard_map/wannier_to_bloch/pallas_call | solution.py:377
  35.1 0.8 %copy.9 = f32[2,2,32,1152]{3,2,1,0:T(8,128)} copy(f32[2,2,32,1152]{3,2,1,0:T(8,128)S(1)} %bitcast.4) | data formatting | bytes 1179648

commit v6 on v5

--- a/solution.py
+++ b/solution.py
@@ -19,7 +19,7 @@
 NEXT = (2, 1, 3, 0)
 EARLY = ((1, 0), (0, 1), (3, 0), (1, 1), (3, 1))
 LATE = ((2, 1), (2, 0))
-EARLY_ROWS = 6
+EARLY_ROWS = 5
 SINE = (6.281640231507743, -41.11355805211909, 73.72054790475445)
 ROUND = 1.5 * 2.0**23
 N_DEV = N_RP * N_PB
@@ -264,14 +264,15 @@
                 device_id=(to_rp, group * N_NEAR + to_near), device_id_type=MESH,
             ).start()
 
+        for j in (4, 5, 2, 3, 6, 7, 1):
+            push(j)
+
         @pl.when((to_rp != rp) | (group != far))
         def _():
             push(0)
 
-        for j in range(1, N_NEAR):
-            push(j)
-
-    for d in (2, 1 + 2 * z, 3 - 2 * z, 0):
+    odd = lax.rem(near // 2 + x + z, 2)
+    for d in (2, 1 + 2 * odd, 3 - 2 * odd, 0):
         group = lax.rem(far + d, N_FAR)
         @pl.when(is_hot)
         def _():

time: 36 us -> 35.9 us (level)
  no operation moved by 1% of the time
where the time goes in v6:
time: 35.9 us; the launch traced here: 35.8 us
  Pallas kernels  34.4 us (96%)
  local copies, waits for them, and re-layouts  0.82 us (2%)
  between operations  0.66 us (2%)
    pallas_call x1, Pallas kernels, local(): pl.pallas_call(kernel, name='wannier_to_bloch', out_shape=pltpu.VMEM((4 *...  34.4 us
    unnamed x1, local copies, waits for them, and re-layouts  0.82 us

profile of v6, /device:TPU:1, one launch (start us, length us, event | category | flops | bytes accessed | tf_op | source)
XLA Modules:
  0.0 35.8 jit_solution(16023433758729479696)
XLA Ops:
  0.7 34.4 %wannier_to_bloch.1 = f32[128,1152]{1,0:T(8,128)S(1)} custom-call(bf16[2,128,1152]{2,1,0:T(8,128)(2,1)} %bitcast.5, s32[3,1024]{1,0:T(4,128)} %rc_hbm.1, s32[2,3]{1,0:T(2,128)} %bitcast.7, s32[1]{0:T(128)S(6)} %copy.10.ki_hbm, bf16[8,2,32,32]{3,2,1,0:T(8,128)(2,1)} %kv_hbm.1, bf16[2,2,32,32]{3,2,1,0:T(8,128)(2,1)} %kq_hbm.1, bf16[2,36,2,36]{3,2,1,0:T(2,128)(2,1)} %bitcast.6), custom_call_target="tpu_custom_call" | custom-call | tf_op jit(solution)/shard_map/wannier_to_bloch/pallas_call | solution.py:378
  35.0 0.8 %copy.9 = f32[2,2,32,1152]{3,2,1,0:T(8,128)} copy(f32[2,2,32,1152]{3,2,1,0:T(8,128)S(1)} %bitcast.4) | data formatting | bytes 1179648
